TPU v7x, 512 devices: a whole 4x8x8 slice. The times are simulated.
512 devices in a mesh: row: 8 (over x, z_hi), col: 16 (over y, core), layer: 4 (over z_lo).
Axes of the slice: x: 4, y: 8, z: 8 (z_hi: 2, z_lo: 4; z = z_hi * 4 + z_lo), core: 2. Of those that a mesh axis runs over, the one named last changes fastest.
Arguments:
- panel: float32 [1024, 8192], P('layer', ('col', 'row')), may hold values from -0.75 to 0.75
- c_in: float32 [16, 8, 64, 8192], P('layer', 'row', None, 'col'), may hold values from -1.5 to 1.5
Outputs:
- updated: float32 [16, 8, 64, 8192], P('layer', 'row', None, 'col')
All inputs are finite; a program needn't handle non-finite values.
Results may differ from a plain program's by a relative error of at most 0.000062.
Values sent between devices are 32-bit elements; how exact they have to be, the bound alone decides.
A program may use at most 64 MiB of HBM per device.

v0:
```python
import jax
import jax.numpy as jnp
from jax import lax
from jax.sharding import Mesh
from jax.sharding import PartitionSpec as P

COL = ("col_0", "col_1")
COL_ROW = ("col_0", "col_1", "row")


def gather_axes(value, axes, dim):
    if not axes:
        return value
    nearer = lax.all_gather(value, axes[-1], axis=dim, tiled=True)
    return gather_axes(nearer, axes[:-1], dim)


def copy_for_each(value, axis):
    length = lax.axis_size(axis)
    return lax.all_to_all(
        jnp.broadcast_to(value[None], (length, *value.shape)), axis, 0, 0, tiled=True
    )


def in_order(blocks, dim):
    dims = list(blocks.shape[1:])
    dims[dim] *= blocks.shape[0]
    return jnp.moveaxis(blocks, 0, dim).reshape(dims)


def collect(value, axis, dim):
    blocks = copy_for_each(value, axis)
    return in_order(blocks, dim)


def cut_along(value, dim, length):
    dims = value.shape
    blocks = value.reshape(*dims[:dim], length, dims[dim] // length, *dims[dim + 1 :])
    return jnp.moveaxis(blocks, dim, 0)


def summed_on_arrival(value, axis, dim):
    length = lax.axis_size(axis)
    blocks = lax.all_to_all(cut_along(value, dim, length), axis, 0, 0, tiled=True)
    return jnp.sum(blocks, axis=0)


def product(left, right):
    return lax.dot_general(
        left,
        right,
        (((0,), (0,)), ((), ())),
        precision=lax.Precision.HIGHEST,
        preferred_element_type=jnp.float32,
    )


def on_device(panel, c_in):
    narrow = c_in.shape[2]
    spread = gather_axes(panel, COL, 1)
    local = collect(panel, "row", 1)
    pairs = (spread, local)
    columns_here = pairs[1].shape[1]
    count = c_in.shape[0] * lax.axis_size("layer")
    spread, local = pairs
    total = product(spread, local)
    summed = summed_on_arrival(total.reshape(count, 1, narrow, columns_here), "layer", 0)
    return c_in + summed


def solution(mesh):
    torus = Mesh(
        mesh.devices.reshape(mesh.shape["row"], 8, 2, mesh.shape["layer"]),
        ("row", "col_0", "col_1", "layer"),
    )
    return jax.shard_map(
        on_device,
        mesh=torus,
        in_specs=(P("layer", COL_ROW), P("layer", "row", None, COL)),
        out_specs=P("layer", "row", None, COL),
        check_vma=False,
    )
```

profile of v0, /device:TPU:2, one launch (start us, length us, event | category | flops | bytes accessed | tf_op | source)
XLA Modules:
  0.0 115.5 jit_solution(10263122104835376186)
XLA Ops:
  6.5 0.0 all-gather.2.cloned.1.call-start
  6.5 3.3 %all_gather.6 = f32[256,128]{0,1:T(8,128)} all-gather(f32[256,64]{0,1:T(8,128)} %param.2), channel_id=1, replica_groups=mesh['row'=8,'col_0'=8,'col_1'=2,'layer'=4] {'col_1'}, dimensions={1}, use_global_device_ids=true | all-gather | bytes 196608 | tf_op jit(solution)/shard_map/all_gather | solution.py:14
  9.9 0.0 all-gather.2.cloned.1.call-update
  9.9 0.9 broadcast_in_dim.2
  10.8 30.5 %all_to_all.10 = f32[8,256,64]{1,2,0:T(8,128)S(1)} all-to-all(f32[8,256,64]{1,2,0:T(8,128)S(1)} %broadcast_in_dim.2), channel_id=1, replica_groups=mesh['row'=8,'col_0'=8,'col_1'=2,'layer'=4] {'row'}, dimensions={0} | all-to-all | bytes 1048576 | tf_op jit(solution)/shard_map/all_to_all | solution.py:20
  41.3 14.1 %all-gather.2.cloned.1.call-done = f32[256,1024]{0,1:T(8,128)} async-done(((f32[256,128]{0,1:T(8,128)}), f32[256,1024]{0,1:T(8,128)}) %all-gather.2.cloned.1.call-update) | async-done | bytes 1048592 | tf_op jit(solution)/shard_map/all_gather | solution.py:14
  55.4 3.1 %convolution_bitcast_fusion = f32[4,4,1,64,512]{4,3,1,2,0:T(8,128)S(1)} fusion(f32[4,4,64,256]{3,2,1,0:T(8,128)} %bitcast.17, f32[256,512,1,1]{0,1,3,2:T(8,128)S(1)} %bitcast.16), kind=kOutput, calls=%fused_computation | convolution fusion | flops 1610612736 | bytes 3670016 | tf_op jit(solution)/shard_map/dot_general | solution.py:49
  58.5 48.3 %all_to_all.11 = f32[4,4,1,64,512]{4,3,1,2,0:T(8,128)S(1)} all-to-all(f32[4,4,1,64,512]{4,3,1,2,0:T(8,128)S(1)} %convolution_bitcast_fusion), channel_id=1, replica_groups=mesh['row'=8,'col_0'=8,'col_1'=2,'layer'=4] {'layer'}, dimensions={0} | all-to-all | bytes 4194304 | tf_op jit(solution)/shard_map/all_to_all | solution.py:44
  106.8 0.0 copy-start
  106.8 0.2 reduce_sum.11
  107.0 0.8 copy-done
  107.8 0.9 bitcast_add_fusion
Async XLA Ops:
  6.5 48.9 %all-gather.2.cloned.1.call-start = ((), (), s32[]{:S(2)}) async-start(), calls=%async_computation.2 | async-start | bytes 1179648 | tf_op jit(solution)/shard_map/all_gather | solution.py:14
  106.8 1.0 copy-start
Sparse Core Ops, SparseCore 0:
  10.0 45.3 all-gather.1
where the time goes:
time: 116 us
  blocking collectives  82.1 us (71%)
  waiting for transfers between devices  14.1 us (12%)
  between operations  13.4 us (12%)
  matrix products  3.06 us (3%)
  local copies, waits for them, and re-layouts  1.68 us (1%)
    all_to_all x1, blocking collectives, summed_on_arrival(): lax.all_to_all(cut_along(value, dim, length), axis, 0, 0, tiled=True)  48.3 us
    all_to_all x1, blocking collectives, copy_for_each(): lax.all_to_all(jnp.broadcast_to(value[None], (length, *value.shape)), axi...  30.5 us
    all_gather x1, waiting for transfers between devices, gather_axes(): nearer = lax.all_gather(value, axes[-1], axis=dim, tiled=True)  14.1 us
    all_gather x1, blocking collectives, gather_axes(): nearer = lax.all_gather(value, axes[-1], axis=dim, tiled=True)  3.35 us
    dot_general x1, matrix products, product(): lax.dot_general(left, right, (((0,), (0,)), ((), ())), precision=lax.Prec...  3.06 us
  transfers between devices with their start and end apart: 1, of which 1 were waited for; matrix products, arithmetic and copies ran while one was open for 1% of the time, Pallas kernels for 0%

commit v1 on v0

v1 whole, which is shorter than its diff:
```python
import functools

import jax
import jax.numpy as jnp
from jax import lax
from jax.experimental import pallas as pl
from jax.experimental.pallas import tpu as pltpu
from jax.sharding import Mesh
from jax.sharding import PartitionSpec as P

NX, NY, NZ, NL = 4, 8, 8, 4
W, DEPTH = 64, 256
HALF = W // 2
C0 = 0
Y0 = 32
D0 = 35
Q0 = 39
P0 = 43
SLOTS = 51
RZ, RXP, RXM, RXA, RXB, RY, RD, RQA, RQB, RP, SEMS = 0, 8, 16, 24, 32, 40, 43, 47, 51, 55, 63


def kernel(panel_ref, out_ref, buf, left, send, recv, ready):
    x, zh, y = lax.axis_index("x"), lax.axis_index("zh"), lax.axis_index("y")
    core, zl = lax.axis_index("core"), lax.axis_index("zl")
    z = zh * NL + zl
    q = y % 2
    xp, xm = (x + 1) % NX, (x + NX - 1) % NX
    bar = pltpu.get_barrier_semaphore()

    def on_x(t):
        return {"x": t}

    def on_y(d):
        return {"y": (y + NY + d) % NY}

    def on_z(t):
        return {"zh": t // NL, "zl": t % NL}

    other = {"core": 1 - core}

    def signal(sem, where):
        pl.semaphore_signal(sem, inc=1, device_id=where, device_id_type=pl.DeviceIdType.MESH)

    for where in (on_x(xp), on_x(xm), on_y(1), on_y(-1), on_y(2), on_y(-2), on_y(4), other):
        signal(bar, where)
    for t in range(NZ):

        @pl.when(t > z)
        def _():
            signal(bar, on_z(t))

    def column_slot(i, t):
        return C0 + (t % NL) * 2 * NX + i * 2 + t // NL

    mine = column_slot(x, z)
    buf[mine] = panel_ref[...]

    pl.semaphore_wait(bar, 8 + z)
    for t in range(NZ):

        @pl.when(t < z)
        def _():
            signal(ready.at[z], on_z(t))

    def copy(src, dst, sem, where, part=None):
        a, b = buf.at[src], buf.at[dst]
        if part is not None:
            a, b = a.at[pl.ds(part * HALF, HALF)], b.at[pl.ds(part * HALF, HALF)]
        return pltpu.make_async_remote_copy(
            src_ref=a,
            dst_ref=b,
            send_sem=send.at[sem],
            recv_sem=recv.at[sem],
            device_id=where,
            device_id_type=pl.DeviceIdType.MESH,
        )

    def arrived(dst, sem, part=None):
        copy(dst, dst, sem, other, part).wait_recv()

    def z_copy(t):
        return pltpu.make_async_remote_copy(
            src_ref=panel_ref,
            dst_ref=buf.at[mine],
            send_sem=send.at[RZ + t],
            recv_sem=recv.at[RZ + z],
            device_id=on_z(t),
            device_id_type=pl.DeviceIdType.MESH,
        )

    def z_send(t):
        @pl.when(t > z)
        def _():
            pl.semaphore_wait(ready.at[t], 1)
            z_copy(t).start()

    def x_spread(t):
        slot = column_slot(x, t)
        copy(slot, slot, RXP + t, on_x(xp)).start()
        copy(slot, slot, RXM + t, on_x(xm)).start()

    def x_first(t):
        arrived(column_slot(x, t), RZ + t)
        x_spread(t)

    def x_second(t):
        slot = column_slot(xm, t)
        arrived(slot, RXP + t)
        copy(slot, slot, RXA + t, on_x(xp), 0).start()
        slot = column_slot(xp, t)
        arrived(slot, RXM + t)
        copy(slot, slot, RXB + t, on_x(xm), 1).start()

    def x_last(t):
        slot = column_slot((x + 2) % NX, t)
        arrived(slot, RXA + t, 0)
        arrived(slot, RXB + t, 1)

    def y_home(j):
        return ((y + NY - 2 * j) % NY) // 2

    def y_send():
        for j in (1, 2, 3):
            copy(mine, Y0 + j - 1, RY + j - 1, on_y(2 * j)).start()

    def d_copy(j, home):
        return pltpu.make_async_remote_copy(
            src_ref=buf.at[Y0 + j - 1],
            dst_ref=buf.at[D0 + zl],
            send_sem=send.at[RD + j - 1],
            recv_sem=recv.at[RD + zl],
            device_id=on_z(zh * NL + home),
            device_id_type=pl.DeviceIdType.MESH,
        )

    def y_forward():
        for j in (1, 2, 3):
            arrived(Y0 + j - 1, RY + j - 1)
            home = y_home(j)

            @pl.when(home != zl)
            def _():
                d_copy(j, home).start()

    back = ((y + NY - 2 * zl - q) % NY) // 2
    at_home = back == 0

    def row_slot(layer):
        away = jnp.where(zl == layer, Y0 + back - 1, D0 + layer)
        return jnp.where(at_home, column_slot(x, zh * NL + layer), away)

    def d_forward(layer):
        @pl.when(jnp.logical_and(back != 0, zl != layer))
        def _():
            arrived(D0 + layer, RD + layer)

        slot = row_slot(layer)
        copy(slot, Q0 + layer, RQA + layer, on_y(1), 0).start()
        copy(slot, Q0 + layer, RQB + layer, on_y(-1), 1).start()
        p_copy(slot, q, layer).start()

    def p_copy(slot, parity, layer):
        return copy(slot, P0 + parity * NL + layer, RP + parity * NL + layer, other)

    def q_forward(layer):
        arrived(Q0 + layer, RQA + layer, 0)
        arrived(Q0 + layer, RQB + layer, 1)
        p_copy(Q0 + layer, 1 - q, layer).start()

    for t in range(NZ):

        @pl.when(t < z)
        def _():
            z_copy(t).start()

    x_spread(z)
    y_send()
    near = [(zl + k) % NL for k in (1, 2, 3)]

    @pl.when(zh == 0)
    def _():
        for t in near:
            z_send(t)
        x_second(z)
        for t in near:
            x_first(t)
        y_forward()
        for t in near:
            x_second(t)
        for layer in range(NL):
            d_forward(layer)
        for t in range(NL, NZ):
            z_send(t)
        for t in range(NL, NZ):
            x_first(t)
        for layer in range(NL):
            q_forward(layer)
        for t in range(NL, NZ):
            x_second(t)

    @pl.when(zh == 1)
    def _():
        for t in near:
            z_send(NL + t)
        for t in range(NL):
            x_first(t)
        x_second(z)
        for t in near:
            x_first(NL + t)
        y_forward()
        for t in range(NL):
            x_second(t)
        for layer in range(NL):
            d_forward(layer)
        for t in near:
            x_second(NL + t)
        for layer in range(NL):
            q_forward(layer)

    for parity in (0, 1):
        for layer in range(NL):
            arrived(P0 + parity * NL + layer, RP + parity * NL + layer)
    for t in range(NZ):
        x_last(t)

    for layer in range(NL):
        for parity in (0, 1):
            own = jnp.where(q == parity, row_slot(layer), Q0 + layer)
            theirs = P0 + parity * NL + layer
            a = buf[jnp.where(core == 0, own, theirs)]
            b = buf[jnp.where(core == 0, theirs, own)]
            left[pl.ds(parity * 2 * W, W), :] = a
            left[pl.ds(parity * 2 * W + W, W), :] = b
        right = buf[pl.ds(C0 + layer * 2 * NX, 2 * NX)].reshape(2 * NX * W, DEPTH)
        part = lax.dot_general(
            left[...],
            right,
            (((1,), (1,)), ((), ())),
            precision=lax.Precision.HIGHEST,
            preferred_element_type=jnp.float32,
        )
        if layer == 0:
            out_ref[...] = part
        else:
            out_ref[...] += part

    def sent(src, sem, part=None):
        copy(src, src, sem, other, part).wait_send()

    for t in range(NZ):

        @pl.when(t != z)
        def _():
            sent(mine, RZ + t)

        sent(mine, RXP + t)
        sent(mine, RXM + t)
        sent(mine, RXA + t, 0)
        sent(mine, RXB + t, 1)
    for j in (1, 2, 3):
        sent(mine, RY + j - 1)

        @pl.when(y_home(j) != zl)
        def _():
            sent(mine, RD + j - 1)

    for layer in range(NL):
        sent(mine, RQA + layer, 0)
        sent(mine, RQB + layer, 1)
        for parity in (0, 1):
            sent(mine, RP + parity * NL + layer)


def on_device(panel, c_in):
    gram = pl.pallas_call(
        kernel,
        out_shape=jax.ShapeDtypeStruct((256, 512), jnp.float32),
        in_specs=[pl.BlockSpec(memory_space=pltpu.VMEM)],
        out_specs=pl.BlockSpec(memory_space=pltpu.VMEM),
        scratch_shapes=[
            pltpu.VMEM((SLOTS, W, DEPTH), jnp.float32),
            pltpu.VMEM((4 * W, DEPTH), jnp.float32),
            pltpu.SemaphoreType.DMA((SEMS,)),
            pltpu.SemaphoreType.DMA((SEMS,)),
            pltpu.SemaphoreType.REGULAR((NZ,)),
        ],
        compiler_params=pltpu.CompilerParams(collective_id=0, has_side_effects=True),
        name="gram",
    )(panel.T)
    return c_in + gram.reshape(c_in.shape)


def solution(mesh):
    torus = Mesh(
        mesh.devices.reshape(NX, 2, NY, 2, NL),
        ("x", "zh", "y", "core", "zl"),
    )
    return jax.shard_map(
        on_device,
        mesh=torus,
        in_specs=(
            P("zl", ("y", "core", "x", "zh")),
            P("zl", ("x", "zh"), None, ("y", "core")),
        ),
        out_specs=P("zl", ("x", "zh"), None, ("y", "core")),
        check_vma=False,
    )
```

time: 116 us -> 53 us (0.46)
  the two profiles are of different devices: /device:TPU:2 before, /device:TPU:504 now
where the time goes in v1:
time: 53 us; the launch traced here: 52.8 us
  Pallas kernels  50.8 us (96%)
  other arithmetic  1.91 us (4%)
    pallas_call x1, Pallas kernels, on_device(): pl.pallas_call(kernel, out_shape=jax.ShapeDtypeStruct((256, 512), jnp.flo...  50.8 us
    add x1, other arithmetic, on_device(): return c_in + gram.reshape(c_in.shape)  1.91 us

profile of v1, /device:TPU:504, one launch (start us, length us, event | category | flops | bytes accessed | tf_op | source)
XLA Modules:
  0.0 52.8 jit_solution(2143992356907717603)
XLA Ops:
  0.0 0.0 copy-start
  0.0 50.8 %gram.1 = f32[256,512]{1,0:T(8,128)} custom-call(f32[64,256]{1,0:T(8,128)} %bitcast.5), custom_call_target="tpu_custom_call" | custom-call | tf_op jit(solution)/shard_map/gram/pallas_call | solution.py:276
  50.9 0.0 copy-done
  50.9 1.9 %add.3 = f32[4,1,64,512]{3,2,1,0:T(8,128)} add(f32[4,1,64,512]{3,2,1,0:T(8,128)S(1)} %copy-done, f32[4,1,64,512]{3,2,1,0:T(8,128)} %bitcast.4) | non-fusion elementwise | flops 131072 | bytes 1572864 | tf_op jit(solution)/shard_map/add | solution.py:291
Async XLA Ops:
  0.0 50.9 %copy-start = (f32[4,1,64,512]{3,2,1,0:T(8,128)S(1)}, f32[4,1,64,512]{3,2,1,0:T(8,128)}, u32[]{:S(2)}) copy-start(f32[4,1,64,512]{3,2,1,0:T(8,128)} %param.3) | copy-start | bytes 1572868

commit v2 on v0

v2 whole, which is shorter than its diff:
```python
import functools

import jax
import jax.numpy as jnp
from jax import lax
from jax.experimental import pallas as pl
from jax.experimental.pallas import tpu as pltpu
from jax.sharding import Mesh
from jax.sharding import PartitionSpec as P

NX, NY, NZ, NL = 4, 8, 8, 4
W, DEPTH = 64, 256
C0 = 0
Y0 = 32
D0 = 35
Q0 = 39
P0 = 43
SLOTS = 51
RZ, RX, RY, RD, RQ, DONE, ARRIVALS = 0, 8, 16, 19, 23, 27, 28
LAST_HOPS = 24
DEPARTURES = 4
NEXT, LAST, FAR, SIGNALS = 8, 9, 10, 11

ORDER = (
    (90, 91, 92, 11, 93, 12, 30, 21, 13, 61, 63, 22, 41, 15, 62, 70, 17, 23, 32, 80, 27, 43, 71, 26, 25, 47, 24, 36, 81, 72, 73, 45, 34, 82, 83),
    (90, 91, 92, 12, 93, 13, 41, 20, 22, 61, 63, 14, 30, 23, 32, 17, 62, 71, 43, 70, 24, 81, 80, 72, 27, 34, 73, 26, 25, 82, 83, 47, 36, 45),
    (90, 91, 92, 13, 93, 32, 21, 14, 61, 63, 23, 20, 41, 17, 62, 72, 43, 30, 24, 82, 73, 70, 25, 71, 27, 26, 34, 80, 83, 81, 45, 47, 36),
    (90, 91, 92, 93, 43, 14, 22, 61, 63, 16, 21, 24, 32, 62, 73, 25, 26, 34, 41, 83, 45, 20, 72, 70, 71, 82, 36, 30, 80, 81, 27, 47),
    (90, 91, 92, 15, 93, 16, 34, 23, 17, 61, 63, 25, 22, 43, 62, 70, 26, 45, 32, 27, 21, 36, 80, 71, 47, 72, 41, 20, 81, 73, 82, 30, 83),
    (90, 91, 92, 16, 93, 17, 45, 24, 61, 63, 26, 34, 62, 71, 27, 36, 23, 47, 20, 81, 22, 70, 72, 43, 21, 30, 73, 32, 82, 80, 41, 83),
    (90, 91, 92, 17, 93, 36, 25, 61, 63, 27, 24, 45, 62, 72, 47, 34, 20, 23, 71, 82, 21, 70, 73, 30, 22, 81, 43, 80, 83, 41, 32),
    (90, 91, 92, 93, 47, 20, 26, 61, 63, 25, 21, 62, 73, 22, 30, 36, 24, 45, 72, 41, 71, 83, 70, 32, 23, 81, 82, 80, 34, 43),
)
CROSS = ((7, 5), (7, 4), (7, 4), (4, 6), (3, 1), (0, 3), (0, 3), (0, 2),)
PASS = (
    ((5, (1,)), (6, (1,)), (7, (1,))),
    ((4, (0,)),),
    ((7, (3,)),),
    ((4, (2,)), (5, (2,)), (6, (2,))),
    ((1, (5,)), (2, (5,)), (3, (5,))),
    ((0, (4,)),),
    ((3, (7,)),),
    ((0, (6,)), (1, (6,)), (2, (6,))),
)


def kernel(panel_ref, out_ref, buf, left, acc, send, recv, ready, load):
    x, zh, y = lax.axis_index("x"), lax.axis_index("zh"), lax.axis_index("y")
    core, zl = lax.axis_index("core"), lax.axis_index("zl")
    z = zh * NL + zl
    q = y % 2
    xp, xm = (x + 1) % NX, (x + NX - 1) % NX
    bar = pltpu.get_barrier_semaphore()

    def on_x(t):
        return {"x": t}

    def on_y(d):
        return {"y": (y + NY + d) % NY}

    def on_z(t):
        return {"zh": t // NL, "zl": t % NL}

    other = {"core": 1 - core}

    def signal(sem, where):
        pl.semaphore_signal(sem, inc=1, device_id=where, device_id_type=pl.DeviceIdType.MESH)

    def column_slot(i, t):
        return C0 + t * NX + i

    for where in (on_x(xp), on_x(xm), on_y(1), on_y(-1), other):
        signal(bar, where)
    for t in range(NZ):

        @pl.when(t > z)
        def _():
            signal(bar, on_z(t))

    mine = column_slot(x, z)
    fetch = pltpu.make_async_copy(panel_ref, buf.at[mine], load)
    fetch.start()
    pl.semaphore_wait(bar, 5 + z)
    for t in range(NZ):

        @pl.when(t < z)
        def _():
            signal(ready.at[z], on_z(t))

    signal(ready.at[NEXT], on_y(-1))
    signal(ready.at[LAST], on_y(1))
    fetch.wait()

    def copy(src, dst, to, where, leave=0):
        return pltpu.make_async_remote_copy(
            src_ref=buf.at[src],
            dst_ref=buf.at[dst],
            send_sem=send.at[leave],
            recv_sem=recv.at[to],
            device_id=where,
            device_id_type=pl.DeviceIdType.MESH,
        )

    def arrived(to):
        copy(0, 0, to, other).wait_recv()

    def all_of(count):
        part = buf.at[pl.ds(0, count)]
        return pltpu.make_async_remote_copy(
            src_ref=part,
            dst_ref=part,
            send_sem=send.at[0],
            recv_sem=recv.at[DONE],
            device_id=other,
            device_id_type=pl.DeviceIdType.MESH,
        )

    def z_copy(block, t):
        slot = column_slot(x, block)
        return copy(slot, slot, RZ + block, {"zh": t // NL, "zl": t % NL})

    def x_spread(t):
        slot = column_slot(x, t)
        copy(slot, slot, DONE if t % 2 else RX + t, on_x(xp)).start()
        copy(slot, slot, RX + t if t % 2 else DONE, on_x(xm)).start()

    def x_on(t):
        arrived(RX + t)
        slot = column_slot(xp if t % 2 else xm, t)
        copy(slot, slot, DONE, on_x(xm if t % 2 else xp)).start()

    def y_send(j):
        copy(mine, Y0 + j - 1, RY + j - 1, on_y(2 * j)).start()

    def y_home(j):
        return ((y + NY - 2 * j) % NY) // 2

    def d_copy(j):
        return copy(Y0 + j - 1, D0 + zl, RD + zl, on_z(zh * NL + y_home(j)), j)

    def y_forward(j):
        arrived(RY + j - 1)

        @pl.when(y_home(j) != zl)
        def _():
            d_copy(j).start()

    back = ((y + NY - 2 * zl - q) % NY) // 2

    def row_slot(layer):
        away = jnp.where(zl == layer, Y0 + back - 1, D0 + layer)
        return jnp.where(back == 0, column_slot(x, zh * NL + layer), away)

    def p_copy(slot, parity, layer):
        return copy(slot, P0 + parity * NL + layer, DONE, other)

    def d_forward(layer):
        @pl.when(jnp.logical_and(back != 0, zl != layer))
        def _():
            arrived(RD + layer)

        slot = row_slot(layer)
        copy(slot, Q0 + layer, RQ + layer, on_y(-1 if layer % 2 else 1)).start()
        p_copy(slot, q, layer).start()

    def q_forward(layer):
        arrived(RQ + layer)
        p_copy(Q0 + layer, 1 - q, layer).start()

    def program(place):
        here = place // NL * NL
        near = [t for t in range(here, here + NL) if t != place]
        near.sort(key=lambda t: abs(t - place))
        met = set(range(place + 1))
        count = 3 * NZ + 3 + 12 + len(near) + len(CROSS[place]) + sum(len(to) for _, to in PASS[place])

        def meet(t):
            if t not in met:
                met.add(t)
                pl.semaphore_wait(ready.at[t], 1)

        for t in list(CROSS[place]) + near if here else near:
            if t < place:
                z_copy(place, t).start()
        x_spread(place)
        for code in ORDER[place]:
            step, t = code // 10, code % 10
            if step == 1:
                meet(t)
                z_copy(place, t).start()
            elif step == 2:
                arrived(RZ + t)
                for block, places in PASS[place]:
                    if block == t:
                        for to in places:
                            meet(to)
                            z_copy(block, to).start()
                x_spread(t)
            elif step in (3, 4):
                x_on(t)
            elif step == 6:
                for n in near:
                    meet(n)
                y_forward(t)
            elif step == 7:
                d_forward(t)
            elif step == 8:
                q_forward(t)
            elif t == 0:
                pl.semaphore_wait(ready.at[LAST], 1)
                y_send(3)
            elif t == 1:
                pl.semaphore_wait(ready.at[NEXT], 1)
                y_send(1)
            elif t == 2:
                signal(ready.at[FAR], on_y(-2))
            else:
                pl.semaphore_wait(ready.at[FAR], 1)
                y_send(2)
        for t in range(NZ):
            meet(t)
        all_of(count).wait_send()

    for place in range(NZ):
        pl.when(z == place)(functools.partial(program, place))

    for j in (1, 2, 3):

        @pl.when(y_home(j) != zl)
        def _():
            d_copy(j).wait_send()

    all_of(LAST_HOPS).wait_recv()

    for layer in range(NL):
        for parity in (0, 1):
            own = jnp.where(q == parity, row_slot(layer), Q0 + layer)
            theirs = P0 + parity * NL + layer
            left[pl.ds(parity * 2 * W, W), :] = buf[jnp.where(core == 0, own, theirs)]
            left[pl.ds(parity * 2 * W + W, W), :] = buf[jnp.where(core == 0, theirs, own)]
        for high in (0, 1):
            right = buf[pl.ds(column_slot(0, high * NL + layer), NX)].reshape(NX * W, DEPTH)
            part = lax.dot_general(
                left[...],
                right,
                (((1,), (1,)), ((), ())),
                precision=lax.Precision.HIGHEST,
                preferred_element_type=jnp.float32,
            )
            if layer == 0:
                acc[high] = part
            else:
                acc[high] += part
    first = lax.broadcasted_iota(jnp.int32, (4 * W, 2 * W), 1) < W
    for i in range(NX // 2):
        low, high = (acc[h, :, pl.ds(i * 2 * W, 2 * W)] for h in (0, 1))
        out_ref[:, pl.ds(i * 4 * W, 2 * W)] = jnp.where(first, low, pltpu.roll(high, W, 1))
        out_ref[:, pl.ds(i * 4 * W + 2 * W, 2 * W)] = jnp.where(first, pltpu.roll(low, W, 1), high)


def on_device(panel, c_in):
    gram = pl.pallas_call(
        kernel,
        out_shape=jax.ShapeDtypeStruct((256, 512), jnp.float32),
        in_specs=[pl.BlockSpec(memory_space=pl.ANY)],
        out_specs=pl.BlockSpec(memory_space=pltpu.VMEM),
        scratch_shapes=[
            pltpu.VMEM((SLOTS, W, DEPTH), jnp.float32),
            pltpu.VMEM((4 * W, DEPTH), jnp.float32),
            pltpu.VMEM((2, 4 * W, NX * W), jnp.float32),
            pltpu.SemaphoreType.DMA((DEPARTURES,)),
            pltpu.SemaphoreType.DMA((ARRIVALS,)),
            pltpu.SemaphoreType.REGULAR((SIGNALS,)),
            pltpu.SemaphoreType.DMA,
        ],
        compiler_params=pltpu.CompilerParams(collective_id=0, has_side_effects=True),
        name="gram",
    )(panel.T)
    return c_in + gram.reshape(c_in.shape)


def solution(mesh):
    torus = Mesh(
        mesh.devices.reshape(NX, 2, NY, 2, NL),
        ("x", "zh", "y", "core", "zl"),
    )
    return jax.shard_map(
        on_device,
        mesh=torus,
        in_specs=(
            P("zl", ("y", "core", "x", "zh")),
            P("zl", ("x", "zh"), None, ("y", "core")),
        ),
        out_specs=P("zl", ("x", "zh"), None, ("y", "core")),
        check_vma=False,
    )
```

time: 116 us -> 39.6 us (0.34)
  the two profiles are of different devices: /device:TPU:2 before, /device:TPU:256 now
where the time goes in v2:
time: 39.6 us; the launch traced here: 39.4 us
  Pallas kernels  37.4 us (94%)
  other arithmetic  1.91 us (5%)
    pallas_call x1, Pallas kernels, on_device(): pl.pallas_call(kernel, out_shape=jax.ShapeDtypeStruct((256, 512), jnp.flo...  37.4 us
    add x1, other arithmetic, on_device(): return c_in + gram.reshape(c_in.shape)  1.91 us

profile of v2, /device:TPU:256, one launch (start us, length us, event | category | flops | bytes accessed | tf_op | source)
XLA Modules:
  0.0 39.4 jit_solution(10284225691584453336)
XLA Ops:
  0.0 0.0 copy-start
  0.0 37.4 %gram.1 = f32[256,512]{1,0:T(8,128)} custom-call(f32[64,256]{1,0:T(8,128)} %bitcast.5), custom_call_target="tpu_custom_call" | custom-call | tf_op jit(solution)/shard_map/gram/pallas_call | solution.py:262
  37.4 0.0 copy-done
  37.5 1.9 %add.3 = f32[4,1,64,512]{3,2,1,0:T(8,128)} add(f32[4,1,64,512]{3,2,1,0:T(8,128)S(1)} %copy-done, f32[4,1,64,512]{3,2,1,0:T(8,128)} %bitcast.4) | non-fusion elementwise | flops 131072 | bytes 1572864 | tf_op jit(solution)/shard_map/add | solution.py:279
Async XLA Ops:
  0.0 37.4 %copy-start = (f32[4,1,64,512]{3,2,1,0:T(8,128)S(1)}, f32[4,1,64,512]{3,2,1,0:T(8,128)}, u32[]{:S(2)}) copy-start(f32[4,1,64,512]{3,2,1,0:T(8,128)} %param.3) | copy-start | bytes 1572868

commit v3 on v2

--- a/solution.py
+++ b/solution.py
@@ -19,17 +19,17 @@
 RZ, RX, RY, RD, RQ, DONE, ARRIVALS = 0, 8, 16, 19, 23, 27, 28
 LAST_HOPS = 24
 DEPARTURES = 4
-NEXT, LAST, FAR, SIGNALS = 8, 9, 10, 11
+NEXT, LAST, FAR, ACROSS, SIGNALS = 8, 9, 10, 11, 12
 
 ORDER = (
-    (90, 91, 92, 11, 93, 12, 30, 21, 13, 61, 63, 22, 41, 15, 62, 70, 17, 23, 32, 80, 27, 43, 71, 26, 25, 47, 24, 36, 81, 72, 73, 45, 34, 82, 83),
-    (90, 91, 92, 12, 93, 13, 41, 20, 22, 61, 63, 14, 30, 23, 32, 17, 62, 71, 43, 70, 24, 81, 80, 72, 27, 34, 73, 26, 25, 82, 83, 47, 36, 45),
-    (90, 91, 92, 13, 93, 32, 21, 14, 61, 63, 23, 20, 41, 17, 62, 72, 43, 30, 24, 82, 73, 70, 25, 71, 27, 26, 34, 80, 83, 81, 45, 47, 36),
-    (90, 91, 92, 93, 43, 14, 22, 61, 63, 16, 21, 24, 32, 62, 73, 25, 26, 34, 41, 83, 45, 20, 72, 70, 71, 82, 36, 30, 80, 81, 27, 47),
-    (90, 91, 92, 15, 93, 16, 34, 23, 17, 61, 63, 25, 22, 43, 62, 70, 26, 45, 32, 27, 21, 36, 80, 71, 47, 72, 41, 20, 81, 73, 82, 30, 83),
-    (90, 91, 92, 16, 93, 17, 45, 24, 61, 63, 26, 34, 62, 71, 27, 36, 23, 47, 20, 81, 22, 70, 72, 43, 21, 30, 73, 32, 82, 80, 41, 83),
-    (90, 91, 92, 17, 93, 36, 25, 61, 63, 27, 24, 45, 62, 72, 47, 34, 20, 23, 71, 82, 21, 70, 73, 30, 22, 81, 43, 80, 83, 41, 32),
-    (90, 91, 92, 93, 47, 20, 26, 61, 63, 25, 21, 62, 73, 22, 30, 36, 24, 45, 72, 41, 71, 83, 70, 32, 23, 81, 82, 80, 34, 43),
+    (90, 91, 92, 93, 11, 30, 12, 21, 13, 61, 63, 17, 15, 62, 70, 22, 41, 80, 32, 27, 23, 26, 25, 71, 47, 72, 43, 24, 81, 36, 73, 45, 34, 82, 83),
+    (90, 91, 92, 12, 93, 13, 41, 20, 22, 61, 63, 14, 17, 30, 23, 32, 62, 71, 70, 43, 24, 81, 80, 72, 27, 34, 26, 25, 73, 82, 47, 36, 45, 83),
+    (90, 91, 92, 13, 93, 32, 21, 14, 61, 63, 23, 17, 20, 41, 62, 72, 43, 30, 82, 24, 70, 73, 71, 25, 27, 26, 34, 80, 83, 45, 81, 47, 36),
+    (90, 91, 92, 93, 14, 43, 22, 16, 61, 63, 24, 32, 21, 25, 62, 73, 26, 34, 41, 72, 83, 45, 20, 70, 82, 36, 71, 80, 30, 27, 81, 47),
+    (90, 91, 92, 15, 16, 93, 17, 34, 23, 25, 61, 63, 22, 43, 26, 62, 70, 45, 27, 21, 32, 80, 71, 36, 72, 81, 20, 47, 41, 73, 82, 30, 83),
+    (90, 91, 92, 16, 93, 17, 45, 24, 61, 63, 26, 34, 62, 71, 27, 36, 23, 81, 47, 20, 22, 72, 70, 43, 21, 30, 73, 32, 80, 82, 41, 83),
+    (90, 91, 92, 17, 93, 36, 25, 27, 61, 63, 24, 45, 62, 72, 47, 34, 20, 23, 82, 71, 21, 73, 30, 70, 43, 22, 81, 83, 80, 41, 32),
+    (90, 91, 92, 93, 47, 20, 61, 63, 26, 21, 25, 30, 62, 73, 22, 36, 41, 24, 45, 72, 83, 71, 23, 82, 70, 32, 81, 34, 43, 80),
 )
 CROSS = ((7, 5), (7, 4), (7, 4), (4, 6), (3, 1), (0, 3), (0, 3), (0, 2),)
 PASS = (
@@ -42,6 +42,19 @@
     ((3, (7,)),),
     ((0, (6,)), (1, (6,)), (2, (6,))),
 )
+PAIR = ((), (), (), (), (), (), (), (),)
+
+
+def product(left, right):
+    def dot(a, b):
+        return lax.dot_general(a, b, (((1,), (1,)), ((), ())), preferred_element_type=jnp.float32)
+
+    def terms(value):
+        high = value.astype(jnp.bfloat16)
+        return high, (value - high.astype(jnp.float32)).astype(jnp.bfloat16)
+
+    (a, c), (b, d) = terms(left), terms(right)
+    return dot(a, b) + (dot(a, d) + dot(c, b))
 
 
 def kernel(panel_ref, out_ref, buf, left, acc, send, recv, ready, load):
@@ -89,6 +102,7 @@
 
     signal(ready.at[NEXT], on_y(-1))
     signal(ready.at[LAST], on_y(1))
+    signal(ready.at[ACROSS], on_x(xp))
     fetch.wait()
 
     def copy(src, dst, to, where, leave=0):
@@ -119,10 +133,13 @@
         slot = column_slot(x, block)
         return copy(slot, slot, RZ + block, {"zh": t // NL, "zl": t % NL})
 
-    def x_spread(t):
+    def x_spread(t, direct):
         slot = column_slot(x, t)
-        copy(slot, slot, DONE if t % 2 else RX + t, on_x(xp)).start()
-        copy(slot, slot, RX + t if t % 2 else DONE, on_x(xm)).start()
+        up, down = (DONE, DONE) if direct else (DONE, RX + t) if t % 2 else (RX + t, DONE)
+        copy(slot, slot, up, on_x(xp)).start()
+        copy(slot, slot, down, on_x(xm)).start()
+        if direct:
+            copy(slot, slot, DONE, on_x((x + 2) % NX)).start()
 
     def x_on(t):
         arrived(RX + t)
@@ -182,7 +199,15 @@
         for t in list(CROSS[place]) + near if here else near:
             if t < place:
                 z_copy(place, t).start()
-        x_spread(place)
+        pair_met = []
+
+        def spread(t):
+            if t in PAIR[place] and not pair_met:
+                pair_met.append(t)
+                pl.semaphore_wait(ready.at[ACROSS], 1)
+            x_spread(t, t in PAIR[place])
+
+        spread(place)
         for code in ORDER[place]:
             step, t = code // 10, code % 10
             if step == 1:
@@ -195,7 +220,7 @@
                         for to in places:
                             meet(to)
                             z_copy(block, to).start()
-                x_spread(t)
+                spread(t)
             elif step in (3, 4):
                 x_on(t)
             elif step == 6:
@@ -219,6 +244,9 @@
                 y_send(2)
         for t in range(NZ):
             meet(t)
+        if not pair_met:
+            pl.semaphore_wait(ready.at[ACROSS], 1)
+        all_of(LAST_HOPS + len(PAIR[place])).wait_recv()
         all_of(count).wait_send()
 
     for place in range(NZ):
@@ -229,8 +257,6 @@
         @pl.when(y_home(j) != zl)
         def _():
             d_copy(j).wait_send()
-
-    all_of(LAST_HOPS).wait_recv()
 
     for layer in range(NL):
         for parity in (0, 1):
@@ -240,13 +266,7 @@
             left[pl.ds(parity * 2 * W + W, W), :] = buf[jnp.where(core == 0, theirs, own)]
         for high in (0, 1):
             right = buf[pl.ds(column_slot(0, high * NL + layer), NX)].reshape(NX * W, DEPTH)
-            part = lax.dot_general(
-                left[...],
-                right,
-                (((1,), (1,)), ((), ())),
-                precision=lax.Precision.HIGHEST,
-                preferred_element_type=jnp.float32,
-            )
+            part = product(left[...], right)
             if layer == 0:
                 acc[high] = part
             else:
@@ -261,7 +281,7 @@
 def on_device(panel, c_in):
     gram = pl.pallas_call(
         kernel,
-        out_shape=jax.ShapeDtypeStruct((256, 512), jnp.float32),
+        out_shape=pltpu.VMEM((256, 512), jnp.float32),
         in_specs=[pl.BlockSpec(memory_space=pl.ANY)],
         out_specs=pl.BlockSpec(memory_space=pltpu.VMEM),
         scratch_shapes=[

time: 39.6 us -> 36.9 us (0.932)
  the two profiles are of different devices: /device:TPU:256 before, /device:TPU:384 now
where the time goes in v3:
time: 36.9 us; the launch traced here: 36.7 us
  Pallas kernels  35.8 us (97%)
  other arithmetic  0.87 us (2%)
    pallas_call x1, Pallas kernels, on_device(): pl.pallas_call(kernel, out_shape=pltpu.VMEM((256, 512), jnp.float32), in_...  35.8 us
    add x1, other arithmetic, on_device(): return c_in + gram.reshape(c_in.shape)  0.87 us

profile of v3, /device:TPU:384, one launch (start us, length us, event | category | flops | bytes accessed | tf_op | source)
XLA Modules:
  0.0 36.7 jit_solution(9311211001331443286)
XLA Ops:
  0.0 0.0 copy-start
  0.0 35.8 %gram.1 = f32[256,512]{1,0:T(8,128)S(1)} custom-call(f32[64,256]{1,0:T(8,128)} %bitcast.5), custom_call_target="tpu_custom_call" | custom-call | tf_op jit(solution)/shard_map/gram/pallas_call | solution.py:282
  35.8 0.0 copy-done
  35.9 0.9 %add.3 = f32[4,1,64,512]{3,2,1,0:T(8,128)} add(f32[4,1,64,512]{3,2,1,0:T(8,128)S(1)} %copy-done, f32[4,1,64,512]{3,2,1,0:T(8,128)S(1)} %bitcast.4) | non-fusion elementwise | flops 131072 | bytes 1572864 | tf_op jit(solution)/shard_map/add | solution.py:299
Async XLA Ops:
  0.0 35.8 %copy-start = (f32[4,1,64,512]{3,2,1,0:T(8,128)S(1)}, f32[4,1,64,512]{3,2,1,0:T(8,128)}, u32[]{:S(2)}) copy-start(f32[4,1,64,512]{3,2,1,0:T(8,128)} %param.3) | copy-start | bytes 1572868

commit v4 on v2

--- a/solution.py
+++ b/solution.py
@@ -16,20 +16,20 @@
 Q0 = 39
 P0 = 43
 SLOTS = 51
-RZ, RX, RY, RD, RQ, DONE, ARRIVALS = 0, 8, 16, 19, 23, 27, 28
-LAST_HOPS = 24
-DEPARTURES = 4
-NEXT, LAST, FAR, SIGNALS = 8, 9, 10, 11
+RZ, RX, RY, RD, RQ, DONE, PAIRED, ARRIVALS = 0, 8, 16, 19, 23, 27, 29, 30
+LAST_HOPS = 8
+UP, DOWN, FARTHER, DEPARTURES = 2, 4, 5, 6
+NEXT, LAST, SIGNALS = 8, 9, 10
 
 ORDER = (
-    (90, 91, 92, 11, 93, 12, 30, 21, 13, 61, 63, 22, 41, 15, 62, 70, 17, 23, 32, 80, 27, 43, 71, 26, 25, 47, 24, 36, 81, 72, 73, 45, 34, 82, 83),
-    (90, 91, 92, 12, 93, 13, 41, 20, 22, 61, 63, 14, 30, 23, 32, 17, 62, 71, 43, 70, 24, 81, 80, 72, 27, 34, 73, 26, 25, 82, 83, 47, 36, 45),
-    (90, 91, 92, 13, 93, 32, 21, 14, 61, 63, 23, 20, 41, 17, 62, 72, 43, 30, 24, 82, 73, 70, 25, 71, 27, 26, 34, 80, 83, 81, 45, 47, 36),
-    (90, 91, 92, 93, 43, 14, 22, 61, 63, 16, 21, 24, 32, 62, 73, 25, 26, 34, 41, 83, 45, 20, 72, 70, 71, 82, 36, 30, 80, 81, 27, 47),
-    (90, 91, 92, 15, 93, 16, 34, 23, 17, 61, 63, 25, 22, 43, 62, 70, 26, 45, 32, 27, 21, 36, 80, 71, 47, 72, 41, 20, 81, 73, 82, 30, 83),
-    (90, 91, 92, 16, 93, 17, 45, 24, 61, 63, 26, 34, 62, 71, 27, 36, 23, 47, 20, 81, 22, 70, 72, 43, 21, 30, 73, 32, 82, 80, 41, 83),
-    (90, 91, 92, 17, 93, 36, 25, 61, 63, 27, 24, 45, 62, 72, 47, 34, 20, 23, 71, 82, 21, 70, 73, 30, 22, 81, 43, 80, 83, 41, 32),
-    (90, 91, 92, 93, 47, 20, 26, 61, 63, 25, 21, 62, 73, 22, 30, 36, 24, 45, 72, 41, 71, 83, 70, 32, 23, 81, 82, 80, 34, 43),
+    (90, 91, 11, 30, 12, 21, 13, 61, 63, 70, 17, 15, 80, 22, 41, 50, 27, 32, 71, 23, 26, 25, 72, 47, 81, 73, 24, 43, 36, 51, 82, 45, 83, 52, 34, 53),
+    (90, 91, 12, 13, 41, 20, 22, 61, 63, 71, 14, 17, 30, 23, 32, 81, 70, 72, 43, 51, 80, 24, 27, 73, 26, 82, 25, 50, 83, 47, 52, 34, 36, 53, 45),
+    (90, 91, 13, 32, 21, 14, 61, 63, 72, 23, 17, 20, 41, 82, 43, 30, 71, 73, 52, 70, 24, 27, 25, 81, 26, 83, 80, 34, 51, 53, 47, 50, 36, 45),
+    (90, 91, 14, 43, 22, 16, 61, 63, 73, 24, 25, 32, 21, 83, 72, 26, 34, 53, 71, 82, 45, 20, 41, 70, 81, 27, 36, 52, 80, 30, 51, 47, 50),
+    (90, 91, 15, 16, 17, 34, 23, 25, 61, 63, 70, 22, 26, 43, 80, 71, 45, 27, 32, 21, 72, 50, 36, 81, 73, 82, 47, 20, 41, 51, 83, 52, 30, 53),
+    (90, 91, 16, 17, 45, 24, 61, 63, 71, 26, 34, 81, 27, 36, 23, 72, 51, 20, 70, 47, 73, 22, 21, 43, 82, 80, 83, 30, 52, 32, 41, 50, 53),
+    (90, 91, 17, 36, 25, 27, 63, 61, 72, 24, 45, 71, 47, 82, 34, 20, 23, 52, 70, 73, 81, 21, 22, 80, 30, 83, 43, 51, 53, 41, 32, 50),
+    (90, 91, 47, 20, 26, 61, 63, 73, 21, 25, 30, 72, 22, 83, 71, 36, 41, 24, 53, 82, 45, 70, 81, 23, 52, 32, 80, 51, 34, 43, 50),
 )
 CROSS = ((7, 5), (7, 4), (7, 4), (4, 6), (3, 1), (0, 3), (0, 3), (0, 2),)
 PASS = (
@@ -44,6 +44,18 @@
 )
 
 
+def product(left, right):
+    def dot(a, b):
+        return lax.dot_general(a, b, (((1,), (1,)), ((), ())), preferred_element_type=jnp.float32)
+
+    def terms(value):
+        high = value.astype(jnp.bfloat16)
+        return high, (value - high.astype(jnp.float32)).astype(jnp.bfloat16)
+
+    (a, c), (b, d) = terms(left), terms(right)
+    return dot(a, b) + (dot(a, d) + dot(c, b))
+
+
 def kernel(panel_ref, out_ref, buf, left, acc, send, recv, ready, load):
     x, zh, y = lax.axis_index("x"), lax.axis_index("zh"), lax.axis_index("y")
     core, zl = lax.axis_index("core"), lax.axis_index("zl")
@@ -104,13 +116,13 @@
     def arrived(to):
         copy(0, 0, to, other).wait_recv()
 
-    def all_of(count):
+    def all_of(count, to=DONE, leave=0):
         part = buf.at[pl.ds(0, count)]
         return pltpu.make_async_remote_copy(
             src_ref=part,
             dst_ref=part,
-            send_sem=send.at[0],
-            recv_sem=recv.at[DONE],
+            send_sem=send.at[leave],
+            recv_sem=recv.at[to],
             device_id=other,
             device_id_type=pl.DeviceIdType.MESH,
         )
@@ -120,14 +132,14 @@
         return copy(slot, slot, RZ + block, {"zh": t // NL, "zl": t % NL})
 
     def x_spread(t):
-        slot = column_slot(x, t)
-        copy(slot, slot, DONE if t % 2 else RX + t, on_x(xp)).start()
-        copy(slot, slot, RX + t if t % 2 else DONE, on_x(xm)).start()
+        slot, done = column_slot(x, t), DONE + t // NL
+        copy(slot, slot, done if t % 2 else RX + t, on_x(xp)).start()
+        copy(slot, slot, RX + t if t % 2 else done, on_x(xm)).start()
 
     def x_on(t):
         arrived(RX + t)
         slot = column_slot(xp if t % 2 else xm, t)
-        copy(slot, slot, DONE, on_x(xm if t % 2 else xp)).start()
+        copy(slot, slot, DONE + t // NL, on_x(xm if t % 2 else xp)).start()
 
     def y_send(j):
         copy(mine, Y0 + j - 1, RY + j - 1, on_y(2 * j)).start()
@@ -145,26 +157,52 @@
         def _():
             d_copy(j).start()
 
-    back = ((y + NY - 2 * zl - q) % NY) // 2
+    even = (y + NY - 2 * zl - q) % NY
+    back = even // 2
+    odd = (even + NY - 1 + 2 * q) % NY
 
     def row_slot(layer):
-        away = jnp.where(zl == layer, Y0 + back - 1, D0 + layer)
+        away = jnp.where(jnp.logical_and(zl == layer, back != 2), Y0 + back - 1, D0 + layer)
         return jnp.where(back == 0, column_slot(x, zh * NL + layer), away)
 
     def p_copy(slot, parity, layer):
-        return copy(slot, P0 + parity * NL + layer, DONE, other)
+        return copy(slot, P0 + parity * NL + layer, PAIRED, other)
+
+    def row_copy(src, dst, to, step, leave):
+        return copy(src, dst, to, on_y(step), leave)
 
     def d_forward(layer):
-        @pl.when(jnp.logical_and(back != 0, zl != layer))
+        @pl.when(back != 2)
+        def _():
+            @pl.when(jnp.logical_and(back != 0, zl != layer))
+            def _():
+                arrived(RD + layer)
+
+            slot = row_slot(layer)
+
+            @pl.when(jnp.logical_or(even == 0, even == 2))
+            def _():
+                row_copy(slot, Q0 + layer, RQ + layer, 1, UP).start()
+
+            @pl.when(jnp.logical_or(even == 0, even == 6))
+            def _():
+                row_copy(slot, Q0 + layer, RQ + layer, -1, DOWN).start()
+
+            p_copy(slot, q, layer).start()
+
+    def d_far(layer):
+        @pl.when(back == 2)
         def _():
             arrived(RD + layer)
-
-        slot = row_slot(layer)
-        copy(slot, Q0 + layer, RQ + layer, on_y(-1 if layer % 2 else 1)).start()
-        p_copy(slot, q, layer).start()
+            p_copy(D0 + layer, q, layer).start()
 
     def q_forward(layer):
         arrived(RQ + layer)
+
+        @pl.when(odd == (5 if layer % 2 else 3))
+        def _():
+            row_copy(Q0 + layer, D0 + layer, RD + layer, -1 if layer % 2 else 1, FARTHER).start()
+
         p_copy(Q0 + layer, 1 - q, layer).start()
 
     def program(place):
@@ -172,7 +210,7 @@
         near = [t for t in range(here, here + NL) if t != place]
         near.sort(key=lambda t: abs(t - place))
         met = set(range(place + 1))
-        count = 3 * NZ + 3 + 12 + len(near) + len(CROSS[place]) + sum(len(to) for _, to in PASS[place])
+        count = 3 * NZ + 2 + 8 + len(near) + len(CROSS[place]) + sum(len(to) for _, to in PASS[place])
 
         def meet(t):
             if t not in met:
@@ -202,6 +240,8 @@
                 for n in near:
                     meet(n)
                 y_forward(t)
+            elif step == 5:
+                d_far(t)
             elif step == 7:
                 d_forward(t)
             elif step == 8:
@@ -209,14 +249,9 @@
             elif t == 0:
                 pl.semaphore_wait(ready.at[LAST], 1)
                 y_send(3)
-            elif t == 1:
+            else:
                 pl.semaphore_wait(ready.at[NEXT], 1)
                 y_send(1)
-            elif t == 2:
-                signal(ready.at[FAR], on_y(-2))
-            else:
-                pl.semaphore_wait(ready.at[FAR], 1)
-                y_send(2)
         for t in range(NZ):
             meet(t)
         all_of(count).wait_send()
@@ -224,33 +259,40 @@
     for place in range(NZ):
         pl.when(z == place)(functools.partial(program, place))
 
-    for j in (1, 2, 3):
+    for j in (1, 3):
 
         @pl.when(y_home(j) != zl)
         def _():
             d_copy(j).wait_send()
 
-    all_of(LAST_HOPS).wait_recv()
-
+    @pl.when(jnp.logical_or(even == 0, even == 2))
+    def _():
+        all_of(NL, leave=UP).wait_send()
+
+    @pl.when(jnp.logical_or(even == 0, even == 6))
+    def _():
+        all_of(NL, leave=DOWN).wait_send()
+
+    @pl.when(jnp.logical_or(odd == 3, odd == 5))
+    def _():
+        all_of(NL // 2, leave=FARTHER).wait_send()
+
+    all_of(LAST_HOPS, PAIRED).wait_recv()
     for layer in range(NL):
         for parity in (0, 1):
             own = jnp.where(q == parity, row_slot(layer), Q0 + layer)
             theirs = P0 + parity * NL + layer
-            left[pl.ds(parity * 2 * W, W), :] = buf[jnp.where(core == 0, own, theirs)]
-            left[pl.ds(parity * 2 * W + W, W), :] = buf[jnp.where(core == 0, theirs, own)]
-        for high in (0, 1):
-            right = buf[pl.ds(column_slot(0, high * NL + layer), NX)].reshape(NX * W, DEPTH)
-            part = lax.dot_general(
-                left[...],
-                right,
-                (((1,), (1,)), ((), ())),
-                precision=lax.Precision.HIGHEST,
-                preferred_element_type=jnp.float32,
-            )
+            left[layer, pl.ds(parity * 2 * W, W), :] = buf[jnp.where(core == 0, own, theirs)]
+            left[layer, pl.ds(parity * 2 * W + W, W), :] = buf[jnp.where(core == 0, theirs, own)]
+    for half in (zh, 1 - zh):
+        all_of(LAST_HOPS, DONE + half).wait_recv()
+        for layer in range(NL):
+            right = buf[pl.ds(column_slot(0, half * NL + layer), NX)].reshape(NX * W, DEPTH)
+            part = product(left[layer], right)
             if layer == 0:
-                acc[high] = part
+                acc[half] = part
             else:
-                acc[high] += part
+                acc[half] += part
     first = lax.broadcasted_iota(jnp.int32, (4 * W, 2 * W), 1) < W
     for i in range(NX // 2):
         low, high = (acc[h, :, pl.ds(i * 2 * W, 2 * W)] for h in (0, 1))
@@ -261,12 +303,12 @@
 def on_device(panel, c_in):
     gram = pl.pallas_call(
         kernel,
-        out_shape=jax.ShapeDtypeStruct((256, 512), jnp.float32),
+        out_shape=pltpu.VMEM((256, 512), jnp.float32),
         in_specs=[pl.BlockSpec(memory_space=pl.ANY)],
         out_specs=pl.BlockSpec(memory_space=pltpu.VMEM),
         scratch_shapes=[
             pltpu.VMEM((SLOTS, W, DEPTH), jnp.float32),
-            pltpu.VMEM((4 * W, DEPTH), jnp.float32),
+            pltpu.VMEM((NL, 4 * W, DEPTH), jnp.float32),
             pltpu.VMEM((2, 4 * W, NX * W), jnp.float32),
             pltpu.SemaphoreType.DMA((DEPARTURES,)),
             pltpu.SemaphoreType.DMA((ARRIVALS,)),

time: 39.6 us -> 36.3 us (0.917)
  Pallas kernels: 37.4 us -> 35.3 us
  other arithmetic: 1.91 us -> 0.87 us
    pallas_call x1, Pallas kernels: 37.4 us -> 35.3 us  [on_device(): pl.pallas_call(kernel, out_shape=pltpu.VMEM((256, 512), jnp.float32), in_...]
    add x1, other arithmetic: 1.91 us -> 0.87 us  [on_device(): return c_in + gram.reshape(c_in.shape)]
where the time goes in v4:
time: 36.3 us; the launch traced here: 36.2 us
  Pallas kernels  35.3 us (97%)
  other arithmetic  0.87 us (2%)
    pallas_call x1, Pallas kernels, on_device(): pl.pallas_call(kernel, out_shape=pltpu.VMEM((256, 512), jnp.float32), in_...  35.3 us
    add x1, other arithmetic, on_device(): return c_in + gram.reshape(c_in.shape)  0.87 us

profile of v4, /device:TPU:256, one launch (start us, length us, event | category | flops | bytes accessed | tf_op | source)
XLA Modules:
  0.0 36.2 jit_solution(1669116402240255352)
XLA Ops:
  0.0 0.0 copy-start
  0.0 35.3 %gram.1 = f32[256,512]{1,0:T(8,128)S(1)} custom-call(f32[64,256]{1,0:T(8,128)} %bitcast.5), custom_call_target="tpu_custom_call" | custom-call | tf_op jit(solution)/shard_map/gram/pallas_call | solution.py:304
  35.3 0.0 copy-done
  35.3 0.9 %add.3 = f32[4,1,64,512]{3,2,1,0:T(8,128)} add(f32[4,1,64,512]{3,2,1,0:T(8,128)S(1)} %copy-done, f32[4,1,64,512]{3,2,1,0:T(8,128)S(1)} %bitcast.4) | non-fusion elementwise | flops 131072 | bytes 1572864 | tf_op jit(solution)/shard_map/add | solution.py:321
Async XLA Ops:
  0.0 35.3 %copy-start = (f32[4,1,64,512]{3,2,1,0:T(8,128)S(1)}, f32[4,1,64,512]{3,2,1,0:T(8,128)}, u32[]{:S(2)}) copy-start(f32[4,1,64,512]{3,2,1,0:T(8,128)} %param.3) | copy-start | bytes 1572868

commit v5 on v4

--- a/solution.py
+++ b/solution.py
@@ -25,10 +25,10 @@
     (90, 91, 11, 30, 12, 21, 13, 61, 63, 70, 17, 15, 80, 22, 41, 50, 27, 32, 71, 23, 26, 25, 72, 47, 81, 73, 24, 43, 36, 51, 82, 45, 83, 52, 34, 53),
     (90, 91, 12, 13, 41, 20, 22, 61, 63, 71, 14, 17, 30, 23, 32, 81, 70, 72, 43, 51, 80, 24, 27, 73, 26, 82, 25, 50, 83, 47, 52, 34, 36, 53, 45),
     (90, 91, 13, 32, 21, 14, 61, 63, 72, 23, 17, 20, 41, 82, 43, 30, 71, 73, 52, 70, 24, 27, 25, 81, 26, 83, 80, 34, 51, 53, 47, 50, 36, 45),
-    (90, 91, 14, 43, 22, 16, 61, 63, 73, 24, 25, 32, 21, 83, 72, 26, 34, 53, 71, 82, 45, 20, 41, 70, 81, 27, 36, 52, 80, 30, 51, 47, 50),
+    (90, 91, 14, 43, 22, 61, 63, 73, 24, 16, 25, 32, 21, 83, 72, 26, 34, 53, 71, 82, 45, 20, 41, 70, 81, 27, 36, 52, 80, 30, 51, 47, 50),
     (90, 91, 15, 16, 17, 34, 23, 25, 61, 63, 70, 22, 26, 43, 80, 71, 45, 27, 32, 21, 72, 50, 36, 81, 73, 82, 47, 20, 41, 51, 83, 52, 30, 53),
     (90, 91, 16, 17, 45, 24, 61, 63, 71, 26, 34, 81, 27, 36, 23, 72, 51, 20, 70, 47, 73, 22, 21, 43, 82, 80, 83, 30, 52, 32, 41, 50, 53),
-    (90, 91, 17, 36, 25, 27, 63, 61, 72, 24, 45, 71, 47, 82, 34, 20, 23, 52, 70, 73, 81, 21, 22, 80, 30, 83, 43, 51, 53, 41, 32, 50),
+    (90, 91, 17, 36, 25, 27, 63, 61, 72, 24, 45, 71, 47, 82, 34, 20, 23, 52, 70, 73, 81, 21, 22, 80, 30, 83, 41, 43, 51, 53, 32, 50),
     (90, 91, 47, 20, 26, 61, 63, 73, 21, 25, 30, 72, 22, 83, 71, 36, 41, 24, 53, 82, 45, 70, 81, 23, 52, 32, 80, 51, 34, 43, 50),
 )
 CROSS = ((7, 5), (7, 4), (7, 4), (4, 6), (3, 1), (0, 3), (0, 3), (0, 2),)

time: 36.3 us -> 36.3 us (level)
  no operation moved by 1% of the time
where the time goes in v5:
time: 36.3 us; the launch traced here: 36.2 us
  Pallas kernels  35.3 us (97%)
  other arithmetic  0.87 us (2%)
    pallas_call x1, Pallas kernels, on_device(): pl.pallas_call(kernel, out_shape=pltpu.VMEM((256, 512), jnp.float32), in_...  35.3 us
    add x1, other arithmetic, on_device(): return c_in + gram.reshape(c_in.shape)  0.87 us

profile of v5, /device:TPU:256, one launch (start us, length us, event | category | flops | bytes accessed | tf_op | source)
XLA Modules:
  0.0 36.2 jit_solution(10660032745027297680)
XLA Ops:
  0.0 0.0 copy-start
  0.0 35.3 %gram.1 = f32[256,512]{1,0:T(8,128)S(1)} custom-call(f32[64,256]{1,0:T(8,128)} %bitcast.5), custom_call_target="tpu_custom_call" | custom-call | tf_op jit(solution)/shard_map/gram/pallas_call | solution.py:304
  35.3 0.0 copy-done
  35.3 0.9 %add.3 = f32[4,1,64,512]{3,2,1,0:T(8,128)} add(f32[4,1,64,512]{3,2,1,0:T(8,128)S(1)} %copy-done, f32[4,1,64,512]{3,2,1,0:T(8,128)S(1)} %bitcast.4) | non-fusion elementwise | flops 131072 | bytes 1572864 | tf_op jit(solution)/shard_map/add | solution.py:321
Async XLA Ops:
  0.0 35.3 %copy-start = (f32[4,1,64,512]{3,2,1,0:T(8,128)S(1)}, f32[4,1,64,512]{3,2,1,0:T(8,128)}, u32[]{:S(2)}) copy-start(f32[4,1,64,512]{3,2,1,0:T(8,128)} %param.3) | copy-start | bytes 1572868

commit v6 on v5

--- a/solution.py
+++ b/solution.py
@@ -210,7 +210,6 @@
         near = [t for t in range(here, here + NL) if t != place]
         near.sort(key=lambda t: abs(t - place))
         met = set(range(place + 1))
-        count = 3 * NZ + 2 + 8 + len(near) + len(CROSS[place]) + sum(len(to) for _, to in PASS[place])
 
         def meet(t):
             if t not in met:
@@ -254,28 +253,9 @@
                 y_send(1)
         for t in range(NZ):
             meet(t)
-        all_of(count).wait_send()
 
     for place in range(NZ):
         pl.when(z == place)(functools.partial(program, place))
-
-    for j in (1, 3):
-
-        @pl.when(y_home(j) != zl)
-        def _():
-            d_copy(j).wait_send()
-
-    @pl.when(jnp.logical_or(even == 0, even == 2))
-    def _():
-        all_of(NL, leave=UP).wait_send()
-
-    @pl.when(jnp.logical_or(even == 0, even == 6))
-    def _():
-        all_of(NL, leave=DOWN).wait_send()
-
-    @pl.when(jnp.logical_or(odd == 3, odd == 5))
-    def _():
-        all_of(NL // 2, leave=FARTHER).wait_send()
 
     all_of(LAST_HOPS, PAIRED).wait_recv()
     for layer in range(NL):
@@ -299,6 +279,31 @@
         out_ref[:, pl.ds(i * 4 * W, 2 * W)] = jnp.where(first, low, pltpu.roll(high, W, 1))
         out_ref[:, pl.ds(i * 4 * W + 2 * W, 2 * W)] = jnp.where(first, pltpu.roll(low, W, 1), high)
 
+    def departed(place):
+        count = 3 * NZ + 2 + 8 + NL - 1 + len(CROSS[place]) + sum(len(to) for _, to in PASS[place])
+        all_of(count).wait_send()
+
+    for place in range(NZ):
+        pl.when(z == place)(functools.partial(departed, place))
+
+    for j in (1, 3):
+
+        @pl.when(y_home(j) != zl)
+        def _():
+            d_copy(j).wait_send()
+
+    @pl.when(jnp.logical_or(even == 0, even == 2))
+    def _():
+        all_of(NL, leave=UP).wait_send()
+
+    @pl.when(jnp.logical_or(even == 0, even == 6))
+    def _():
+        all_of(NL, leave=DOWN).wait_send()
+
+    @pl.when(jnp.logical_or(odd == 3, odd == 5))
+    def _():
+        all_of(NL // 2, leave=FARTHER).wait_send()
+
 
 def on_device(panel, c_in):
     gram = pl.pallas_call(

time: 36.3 us -> 36.3 us (level)
  no operation moved by 1% of the time
where the time goes in v6:
time: 36.3 us; the launch traced here: 36.2 us
  Pallas kernels  35.3 us (97%)
  other arithmetic  0.87 us (2%)
    pallas_call x1, Pallas kernels, on_device(): pl.pallas_call(kernel, out_shape=pltpu.VMEM((256, 512), jnp.float32), in_...  35.3 us
    add x1, other arithmetic, on_device(): return c_in + gram.reshape(c_in.shape)  0.87 us

profile of v6, /device:TPU:256, one launch (start us, length us, event | category | flops | bytes accessed | tf_op | source)
XLA Modules:
  0.0 36.2 jit_solution(17050355323289823753)
XLA Ops:
  0.0 0.0 copy-start
  0.0 35.3 %gram.1 = f32[256,512]{1,0:T(8,128)S(1)} custom-call(f32[64,256]{1,0:T(8,128)} %bitcast.5), custom_call_target="tpu_custom_call" | custom-call | tf_op jit(solution)/shard_map/gram/pallas_call | solution.py:309
  35.3 0.0 copy-done
  35.3 0.9 %add.3 = f32[4,1,64,512]{3,2,1,0:T(8,128)} add(f32[4,1,64,512]{3,2,1,0:T(8,128)S(1)} %copy-done, f32[4,1,64,512]{3,2,1,0:T(8,128)S(1)} %bitcast.4) | non-fusion elementwise | flops 131072 | bytes 1572864 | tf_op jit(solution)/shard_map/add | solution.py:326
Async XLA Ops:
  0.0 35.3 %copy-start = (f32[4,1,64,512]{3,2,1,0:T(8,128)S(1)}, f32[4,1,64,512]{3,2,1,0:T(8,128)}, u32[]{:S(2)}) copy-start(f32[4,1,64,512]{3,2,1,0:T(8,128)} %param.3) | copy-start | bytes 1572868
